TPU v7x, 32 devices: a whole 2x2x4 slice. The times are simulated.
32 devices in a mesh: outer: 4 (over y, x), inner: 8 (over z, core).
Axes of the slice: x: 2, y: 2, z: 4, core: 2. Of those that a mesh axis runs over, the one named last changes fastest.
Arguments:
- queries: bfloat16 [8192, 16, 128], P(('outer', 'inner')), may hold values from -6 to 6
- key_rows: bfloat16 [8192, 16, 128], P(('outer', 'inner')), may hold values from -6 to 6
- value_rows: bfloat16 [8192, 16, 128], P(('outer', 'inner')), may hold values from -6 to 6
- key_scale: bfloat16 [8192, 16], P(('outer', 'inner')), may hold values from 0.5 to 2
- value_scale: bfloat16 [8192, 16], P(('outer', 'inner')), may hold values from 0.5 to 2
- cluster_label: int32 [16, 8192, 1], P(None, ('outer', 'inner')), may hold values from 0 to 127; in each aligned block of 256 rows (0 to 255, 256 to 511, ..., all dimensions but the last counted through in order) at most 4 rows name the same one
Outputs:
- attended: bfloat16 [8192, 16, 128], P(('outer', 'inner'))
Inputs may be any that keep to these rules, and one draw needn't show every extreme that they name: `cluster_label`: among the 256 rows of one device for one head, no label occurs more than 4 times, and some label occurs exactly 4 times.
All inputs are finite; a program needn't handle non-finite values.
Results may differ from a plain program's by a relative error of at most 0.0033.
Values may be sent and summed in bfloat16 or wider, within the bound.
A program may use at most 64 MiB of HBM per device.

v0:
```python
import jax
import jax.numpy as jnp
from jax import lax
from jax.sharding import PartitionSpec as P

COARSE = 16
FINE = 8


def attend(query_block, key_block, value_block, key_factor, value_factor, position):
    factor = query_block.shape[-1] ** (-0.5)
    scores = jnp.dot(query_block, key_block.T, preferred_element_type=jnp.float32)
    scores = scores * (key_factor.astype(jnp.float32) * factor)[None, :]
    visible = (position[None, :] >= 0) & (position[None, :] <= position[:, None])
    highest = jnp.max(jnp.where(visible, scores, jnp.float32(-1e30)), axis=1, keepdims=True)
    unnormed = jnp.where(visible, jnp.exp(scores - highest), jnp.float32(0.0))
    denominator = jnp.sum(unnormed, axis=1)
    weights = (unnormed * value_factor.astype(jnp.float32)[None, :]).astype(jnp.bfloat16)
    numerator = jnp.dot(weights, value_block, preferred_element_type=jnp.float32)
    safe = jnp.where(denominator > 0, denominator, jnp.float32(1.0))
    return (numerator / safe[:, None]).astype(jnp.bfloat16)


def attend_items(query_part, key_part, value_part, key_factor, value_factor, position):
    leading = query_part.shape[:3]
    slots = query_part.shape[3]
    width = query_part.shape[4]
    total = leading[0] * leading[1] * leading[2]

    def single(inputs):
        return attend(*inputs)

    results = lax.map(
        single,
        (
            query_part.reshape(total, slots, width),
            key_part.reshape(total, slots, width),
            value_part.reshape(total, slots, width),
            key_factor.reshape(total, slots),
            value_factor.reshape(total, slots),
            position.reshape(total, slots),
        ),
    )
    return results.reshape(leading + (slots, width))


def shards(queries, key_rows, value_rows, key_scale, value_scale, cluster_label):
    outer_count = lax.axis_size("outer")
    inner_count = lax.axis_size("inner")
    tok_rows, heads, width = queries.shape
    cluster_count = COARSE * FINE
    capacity = max(2, 2 * tok_rows // cluster_count)
    labels = cluster_label[:, :, 0].T
    member = (
        labels[:, :, None] == jnp.arange(cluster_count, dtype=jnp.int32)[None, None, :]
    ).astype(jnp.int32)
    rank = jnp.sum(jnp.cumsum(member, axis=0) * member, axis=2) - 1
    slot = (labels * heads + jnp.arange(heads, dtype=jnp.int32)[None, :]) * capacity + rank
    flat = slot.reshape(-1)
    total = cluster_count * heads * capacity
    item_count = cluster_count * heads // (outer_count * inner_count)
    layout = (outer_count, inner_count, item_count, capacity)
    source = (
        jnp.full((total,), -1, jnp.int32)
        .at[flat]
        .set(jnp.arange(tok_rows * heads, dtype=jnp.int32))
    )
    filled_slot = source >= 0
    source_row = jnp.maximum(source, 0)

    def place(array):
        rows = array.reshape((tok_rows * heads,) + array.shape[2:])
        picked = rows[source_row]
        mask = filled_slot.reshape((total,) + (1,) * (picked.ndim - 1))
        kept = jnp.where(mask, picked, jnp.zeros((), array.dtype))
        return kept.reshape(layout + array.shape[2:])

    device = lax.axis_index("outer") * inner_count + lax.axis_index("inner")
    position_rows = jnp.where(filled_slot, device * tok_rows + source_row // heads, -1).reshape(
        layout
    )
    outgoing = (
        place(queries),
        place(key_rows),
        place(value_rows),
        place(key_scale),
        place(value_scale),
        position_rows,
    )
    arrived = (
        lax.all_to_all(
            lax.all_to_all(outgoing[0], "outer", split_axis=0, concat_axis=3, tiled=True),
            "inner",
            split_axis=1,
            concat_axis=3,
            tiled=True,
        ),
        lax.all_to_all(
            lax.all_to_all(outgoing[1], "outer", split_axis=0, concat_axis=3, tiled=True),
            "inner",
            split_axis=1,
            concat_axis=3,
            tiled=True,
        ),
        lax.all_to_all(
            lax.all_to_all(outgoing[2], "outer", split_axis=0, concat_axis=3, tiled=True),
            "inner",
            split_axis=1,
            concat_axis=3,
            tiled=True,
        ),
        lax.all_to_all(
            lax.all_to_all(outgoing[3], "outer", split_axis=0, concat_axis=3, tiled=True),
            "inner",
            split_axis=1,
            concat_axis=3,
            tiled=True,
        ),
        lax.all_to_all(
            lax.all_to_all(outgoing[4], "outer", split_axis=0, concat_axis=3, tiled=True),
            "inner",
            split_axis=1,
            concat_axis=3,
            tiled=True,
        ),
        lax.all_to_all(
            lax.all_to_all(outgoing[5], "outer", split_axis=0, concat_axis=3, tiled=True),
            "inner",
            split_axis=1,
            concat_axis=3,
            tiled=True,
        ),
    )
    answered = attend_items(*arrived)
    returned = lax.all_to_all(
        lax.all_to_all(answered, "inner", split_axis=3, concat_axis=1, tiled=True),
        "outer",
        split_axis=3,
        concat_axis=0,
        tiled=True,
    )
    rows_back = returned.reshape(total, width)
    return rows_back[flat].reshape(tok_rows, heads, width)


def solution(mesh):
    placed = (
        P(("outer", "inner"), None, None),
        P(("outer", "inner"), None, None),
        P(("outer", "inner"), None, None),
        P(("outer", "inner"), None),
        P(("outer", "inner"), None),
        P(None, ("outer", "inner"), None),
    )
    return jax.shard_map(
        shards,
        mesh=mesh,
        in_specs=placed,
        out_specs=P(("outer", "inner"), None, None),
        check_vma=False,
    )
```

profile of v0, /device:TPU:0, one launch (start us, length us, event | category | flops | bytes accessed | tf_op | source)
XLA Modules:
  0.0 800.3 jit_solution(17688650080071490091)
XLA Ops:
  7.5 15.5 %scatter_custom_fusion = s32[8192]{0:T(1024)S(1)} fusion(s32[4096]{0:T(1024)S(1)} %bitcast.196, s32[4096]{0:T(1024)S(1)} %iota.12, s32[]{:T(128)} %constant.69.clone.1), kind=kCustom, calls=%fused_computation.69 | custom fusion | bytes 32772 | tf_op jit(solution)/shard_map/scatter | solution.py:66
  23.1 50.7 %gather_fusion.3 = bf16[8192]{0:T(1024)(128)(2,1)S(1)} fusion(bf16[4096]{0:T(1024)(128)(2,1)S(1)} %reshape.142, s32[8192]{0:T(1024)S(1)} %maximum_clamp_fusion), kind=kCustom, calls=%fused_computation.3 | custom fusion | bytes 65536 | tf_op jit(solution)/shard_map/gather | solution.py:73
  73.8 50.7 %gather_fusion.2 = bf16[8192]{0:T(1024)(128)(2,1)S(1)} fusion(bf16[4096]{0:T(1024)(128)(2,1)S(1)} %reshape.139, s32[8192]{0:T(1024)S(1)} %maximum_clamp_fusion), kind=kCustom, calls=%fused_computation.2 | custom fusion | bytes 65536 | tf_op jit(solution)/shard_map/gather | solution.py:73
  126.7 5.2 all-to-all-start.6
  134.0 2.6 all-to-all-done.6
  136.6 3.2 all-to-all-start.8
  142.0 2.5 all-to-all-done.8
  144.5 3.3 all-to-all-start
  148.6 3.9 all-to-all-done
  152.5 4.9 all-to-all-start.7
  158.2 4.9 all-to-all-done.7
  163.0 3.3 all-to-all-start.9
  168.0 29.2 %gather_fusion.4 = bf16[8192,128]{1,0:T(8,128)(2,1)} fusion(bf16[4096,128]{1,0:T(8,128)(2,1)S(1)} %bitcast.167, s32[8192]{0:T(1024)S(1)} %maximum_clamp_fusion), kind=kCustom, calls=%fused_computation.4 | custom fusion | bytes 4227072 | tf_op jit(solution)/shard_map/gather | solution.py:73
  197.2 29.2 %gather_fusion.1 = bf16[8192,128]{1,0:T(8,128)(2,1)} fusion(bf16[4096,128]{1,0:T(8,128)(2,1)S(1)} %bitcast.168, s32[8192]{0:T(1024)S(1)} %maximum_clamp_fusion), kind=kCustom, calls=%fused_computation.1 | custom fusion | bytes 4227072 | tf_op jit(solution)/shard_map/gather | solution.py:73
  226.4 29.2 %gather_fusion = bf16[8192,128]{1,0:T(8,128)(2,1)} fusion(bf16[4096,128]{1,0:T(8,128)(2,1)S(1)} %bitcast.169, s32[8192]{0:T(1024)S(1)} %maximum_clamp_fusion), kind=kCustom, calls=%fused_computation | custom fusion | bytes 4227072 | tf_op jit(solution)/shard_map/gather | solution.py:73
  257.7 5.0 all-to-all-start.1
  262.7 5.9 copy_select_fusion
  268.6 30.9 %all_to_all.231 = bf16[4,8,64,4,128]{4,2,3,1,0:T(8,128)(2,1)} all-to-all(bf16[4,8,64,4,128]{4,2,3,1,0:T(8,128)(2,1)} %get-tuple-element.84), channel_id=1, replica_groups=mesh['outer'=4,'inner'=8] {'outer'}, dimensions={0} | all-to-all | bytes 4194304 | tf_op jit(solution)/shard_map/all_to_all | solution.py:106
  299.5 28.1 %all_to_all.232 = bf16[4,8,64,4,128]{4,2,3,1,0:T(8,128)(2,1)} all-to-all(bf16[4,8,64,4,128]{4,2,3,1,0:T(8,128)(2,1)S(1)} %copy-done.6), channel_id=1, replica_groups=mesh['outer'=4,'inner'=8] {'outer'}, dimensions={0} | all-to-all | bytes 4194304 | tf_op jit(solution)/shard_map/all_to_all | solution.py:99
  327.6 3.6 all-to-all-start.2
  331.2 3.2 copy.51
  334.4 19.7 %all-to-all-done.2 = bf16[4,8,64,4,128]{4,2,3,1,0:T(8,128)(2,1)S(1)} async-done(((bf16[4,8,64,4,128]{4,2,3,1,0:T(8,128)(2,1)}), bf16[4,8,64,4,128]{4,2,3,1,0:T(8,128)(2,1)S(1)}, u32[]{:S(2)}, u32[]{:S(2)}) %all-to-all-start.2) | async-done | bytes 2097184 | tf_op jit(solution)/shard_map/all_to_all | solution.py:92
  355.5 4.5 all-to-all-start.11
  360.0 3.2 copy.42
  363.2 45.8 %all-to-all-done.11 = bf16[1,8,64,16,128]{4,2,3,0,1:T(8,128)(2,1)S(1)} async-done(((bf16[1,8,64,16,128]{4,2,3,0,1:T(8,128)(2,1)}), bf16[1,8,64,16,128]{4,2,3,0,1:T(8,128)(2,1)S(1)}, u32[]{:S(2)}, u32[]{:S(2)}) %all-to-all-start.11) | async-done | bytes 2097184 | tf_op jit(solution)/shard_map/all_to_all | solution.py:105
  409.0 4.3 all-to-all-start.5
  413.4 3.2 copy.39
  416.6 45.8 %all-to-all-done.5 = bf16[1,8,64,16,128]{4,2,3,0,1:T(8,128)(2,1)} async-done(((bf16[1,8,64,16,128]{4,2,3,0,1:T(8,128)(2,1)}), bf16[1,8,64,16,128]{4,2,3,0,1:T(8,128)(2,1)}, u32[]{:S(2)}, u32[]{:S(2)}) %all-to-all-start.5) | async-done | bytes 2097184 | tf_op jit(solution)/shard_map/all_to_all | solution.py:98
  462.4 4.6 all-to-all-start.3
  468.2 2.7 copy.58
  470.9 2.9 copy.55
  473.9 42.1 %all-to-all-done.3 = bf16[1,8,64,16,128]{4,2,3,0,1:T(8,128)(2,1)} async-done(((bf16[1,8,64,16,128]{4,2,3,0,1:T(8,128)(2,1)}), bf16[1,8,64,16,128]{4,2,3,0,1:T(8,128)(2,1)}, u32[]{:S(2)}, u32[]{:S(2)}) %all-to-all-start.3) | async-done | bytes 2097184 | tf_op jit(solution)/shard_map/all_to_all | solution.py:91
  516.0 4.3 copy.54
  520.3 178.5 %while.10 = (s32[]{:T(128)}, bf16[64,128,128]{2,1,0:T(8,128)(2,1)}, s32[64,128]{1,0:T(8,128)S(1)}, bf16[64,128,128]{2,1,0:T(8,128)(2,1)}, bf16[64,128,128]{2,1,0...) while((s32[]{:T(128)}, bf16[64,128,128]{2,1,0:T(8,128)(2,1)}, ...), condition=%wide.region_7.8_spmd, body=%wide.region_4.7_spmd.sunk | while | flops 8684034 | bytes 341365 | solution.py:33
  524.2 1.7 fusion.46
  535.3 1.7 fusion.46
  546.5 1.7 fusion.46
  552.0 1.7 fusion.46
  557.6 1.7 fusion.46
  563.2 1.7 fusion.46
  568.8 1.7 fusion.46
  574.4 1.7 fusion.46
  579.9 1.7 fusion.46
  596.7 1.7 fusion.46
  602.2 1.7 fusion.46
  613.4 1.7 fusion.46
  619.0 1.7 fusion.46
  624.5 1.7 fusion.46
  627.3 1.7 fusion.46
  630.1 1.7 fusion.46
  635.7 1.7 fusion.46
  641.3 1.7 fusion.46
  652.4 1.7 fusion.46
  663.6 1.7 fusion.46
  666.4 1.7 fusion.46
  674.7 1.7 fusion.46
  691.5 1.7 fusion.46
  697.1 1.7 fusion.46
  698.7 2.9 copy.76
  701.7 51.5 %all_to_all.233 = bf16[1,1,64,128,128]{4,2,1,0,3:T(8,128)(2,1)S(1)} all-to-all(bf16[1,1,64,128,128]{4,2,1,0,3:T(8,128)(2,1)S(1)} %bitcast.179), channel_id=1, replica_groups=mesh['outer'=4,'inner'=8] {'inner'}, dimensions={3} | all-to-all | bytes 4194304 | tf_op jit(solution)/shard_map/all_to_all | solution.py:136
  754.6 3.6 all-to-all-start.13
  758.3 24.7 %all-to-all-done.13 = bf16[1,8,64,16,128]{4,2,1,0,3:T(8,128)(2,1)S(1)} async-done(((bf16[1,8,64,16,128]{4,2,1,0,3:T(8,128)(2,1)}), bf16[1,8,64,16,128]{4,2,1,0,3:T(8,128)(2,1)S(1)}, u32[]{:S(2)}, u32[]{:S(2)}) %all-to-all-start.13) | async-done | bytes 2097184 | tf_op jit(solution)/shard_map/all_to_all | solution.py:135
  783.2 2.0 copy.62
  785.2 15.0 %gather_fusion.5 = bf16[4096,128]{1,0:T(8,128)(2,1)} fusion(bf16[8192,128]{1,0:T(8,128)(2,1)S(1)} %bitcast.170, s32[4096]{0:T(1024)S(1)} %broadcast_clamp_fusion), kind=kCustom, calls=%fused_computation.5 | custom fusion | bytes 2113536 | tf_op jit(solution)/shard_map/gather | solution.py:143
  (560 shorter events, 160.7 us)
Async XLA Ops:
  0.0 167.9 %copy-start = (bf16[256,16,128]{2,1,0:T(8,128)(2,1)S(1)}, bf16[256,16,128]{2,1,0:T(8,128)(2,1)}, u32[]{:S(2)}) copy-start(bf16[256,16,128]{2,1,0:T(8,128)(2,1)} %param.10) | copy-start | bytes 3145732
  5.7 1.5 copy-start.7
  126.7 9.9 %all-to-all-start.6 = ((bf16[4,2,1024]{2,1,0:T(2,128)(2,1)}), bf16[4,2,1024]{2,1,0:T(2,128)(2,1)S(1)}, u32[]{:S(2)}, u32[]{:S(2)}) async-start(bf16[4,2,1024]{2,1,0:T(2,128)(2,1)} %reshape.218), calls=%async_computation.6 | async-start | bytes 32768 | tf_op jit(solution)/shard_map/all_to_all | solution.py:113
  136.6 7.9 all-to-all-start.8
  144.5 8.0 all-to-all-start
  152.5 10.5 %all-to-all-start.7 = ((bf16[8,2,512]{2,1,0:T(2,128)(2,1)}), bf16[8,2,512]{2,1,0:T(2,128)(2,1)S(1)}, u32[]{:S(2)}, u32[]{:S(2)}) async-start(bf16[8,2,512]{2,1,0:T(2,128)(2,1)} %reshape.220), calls=%async_computation.7 | async-start | bytes 32768 | tf_op jit(solution)/shard_map/all_to_all | solution.py:112
  163.0 94.6 %all-to-all-start.9 = ((bf16[8,2,512]{2,1,0:T(2,128)(2,1)}), bf16[8,2,512]{2,1,0:T(2,128)(2,1)S(1)}, u32[]{:S(2)}, u32[]{:S(2)}) async-start(bf16[8,2,512]{2,1,0:T(2,128)(2,1)} %reshape.224), calls=%async_computation.9 | async-start | bytes 32768 | tf_op jit(solution)/shard_map/all_to_all | solution.py:119
  167.9 29.2 %copy-start.2 = (bf16[256,16,128]{2,1,0:T(8,128)(2,1)S(1)}, bf16[256,16,128]{2,1,0:T(8,128)(2,1)}, u32[]{:S(2)}) copy-start(bf16[256,16,128]{2,1,0:T(8,128)(2,1)} %param.9) | copy-start | bytes 3145732
  197.2 29.2 %copy-start.3 = (bf16[256,16,128]{2,1,0:T(8,128)(2,1)S(1)}, bf16[256,16,128]{2,1,0:T(8,128)(2,1)}, u32[]{:S(2)}) copy-start(bf16[256,16,128]{2,1,0:T(8,128)(2,1)} %param.8) | copy-start | bytes 3145732
  226.4 36.3 %copy-start.5 = (bf16[8192,128]{1,0:T(8,128)(2,1)S(1)}, bf16[8192,128]{1,0:T(8,128)(2,1)}, u32[]{:S(2)}) copy-start(bf16[8192,128]{1,0:T(8,128)(2,1)} %gather_fusion.4) | copy-start | bytes 6291460
  257.7 10.9 %all-to-all-start.1 = ((s32[8,1,1024]{2,1,0:T(1,128)}), s32[8,1,1024]{2,1,0:T(1,128)S(1)}, u32[]{:S(2)}, u32[]{:S(2)}) async-start(s32[8,1,1024]{2,1,0:T(1,128)} %reshape.216), calls=%async_computation.1 | async-start | bytes 65536 | tf_op jit(solution)/shard_map/all_to_all | solution.py:126
  268.6 30.9 %copy-start.6 = (bf16[4,8,64,4,128]{4,2,3,1,0:T(8,128)(2,1)S(1)}, bf16[4,8,64,4,128]{4,2,3,1,0:T(8,128)(2,1)}, u32[]{:S(2)}) copy-start(bf16[4,8,64,4,128]{4,2,3,1,0:T(8,128)(2,1)} %get-tuple-element.85) | copy-start | bytes 6291460
  327.6 26.6 %all-to-all-start.2 = ((bf16[4,8,64,4,128]{4,2,3,1,0:T(8,128)(2,1)}), bf16[4,8,64,4,128]{4,2,3,1,0:T(8,128)(2,1)S(1)}, u32[]{:S(2)}, u32[]{:S(2)}) async-start(bf16[4,8,64,4,128]{4,2,3,1,0:T(8,128)(2,1)} %get-tuple-element.86), calls=%async_computation.2 | async-start | bytes 4194304 | tf_op jit(solution)/shard_map/all_to_all | solution.py:92
  354.2 1.3 copy-start.4
  355.5 53.5 %all-to-all-start.11 = ((bf16[1,8,64,16,128]{4,2,3,0,1:T(8,128)(2,1)}), bf16[1,8,64,16,128]{4,2,3,0,1:T(8,128)(2,1)S(1)}, u32[]{:S(2)}, u32[]{:S(2)}) async-start(bf16[1,8,64,16,128]{4,2,3,0,1:T(8,128)(2,1)} %bitcast.176), calls=%async_computation.11 | async-start | bytes 4194304 | tf_op jit(solution)/shard_map/all_to_all | solution.py:105
  409.0 53.4 %all-to-all-start.5 = ((bf16[1,8,64,16,128]{4,2,3,0,1:T(8,128)(2,1)}), bf16[1,8,64,16,128]{4,2,3,0,1:T(8,128)(2,1)}, u32[]{:S(2)}, u32[]{:S(2)}) async-start(bf16[1,8,64,16,128]{4,2,3,0,1:T(8,128)(2,1)} %bitcast.177), calls=%async_computation.5 | async-start | bytes 4194304 | tf_op jit(solution)/shard_map/all_to_all | solution.py:98
  462.4 53.6 %all-to-all-start.3 = ((bf16[1,8,64,16,128]{4,2,3,0,1:T(8,128)(2,1)}), bf16[1,8,64,16,128]{4,2,3,0,1:T(8,128)(2,1)}, u32[]{:S(2)}, u32[]{:S(2)}) async-start(bf16[1,8,64,16,128]{4,2,3,0,1:T(8,128)(2,1)} %bitcast.172), calls=%async_computation.3 | async-start | bytes 4194304 | tf_op jit(solution)/shard_map/all_to_all | solution.py:91
  754.6 28.4 %all-to-all-start.13 = ((bf16[1,8,64,16,128]{4,2,1,0,3:T(8,128)(2,1)}), bf16[1,8,64,16,128]{4,2,1,0,3:T(8,128)(2,1)S(1)}, u32[]{:S(2)}, u32[]{:S(2)}) async-start(bf16[1,8,64,16,128]{4,2,1,0,3:T(8,128)(2,1)} %bitcast.178), calls=%async_computation.13 | async-start | bytes 4194304 | tf_op jit(solution)/shard_map/all_to_all | solution.py:135
  785.2 15.0 %copy-start.1 = (bf16[256,16,128]{2,1,0:T(8,128)(2,1)S(1)}, bf16[256,16,128]{2,1,0:T(8,128)(2,1)}, u32[]{:S(2)}) copy-start(bf16[256,16,128]{2,1,0:T(8,128)(2,1)} %param.10) | copy-start | bytes 3145732
where the time goes:
time: 810 us; the launch traced here: 800 us
  local copies, waits for them, and re-layouts  264 us (33%)
  waiting for transfers between devices  192 us (24%)
  matrix products  166 us (20%)
  blocking collectives  111 us (14%)
  starting transfers between devices  45.5 us (6%)
  other arithmetic  20.4 us (3%)
    gather x5, local copies, waits for them, and re-layouts, place(): picked = rows[source_row]  189 us
    dot_general x64, matrix products, attend(): jnp.dot(weights, value_block, preferred_element_type=jnp.float32)  106 us
    dot_general x64, matrix products, attend(): jnp.dot(query_block, key_block.T, preferred_element_type=jnp.float32)  60.2 us
    all_to_all x1, blocking collectives, shards(): lax.all_to_all(answered, 'inner', split_axis=3, concat_axis=1, tiled=True)  51.5 us
    all_to_all x1, waiting for transfers between devices, shards(): lax.all_to_all(lax.all_to_all(outgoing[2], 'outer', split_axis=0, concat_...  45.8 us
    all_to_all x1, waiting for transfers between devices, shards(): lax.all_to_all(lax.all_to_all(outgoing[1], 'outer', split_axis=0, concat_...  45.8 us
    all_to_all x1, waiting for transfers between devices, shards(): lax.all_to_all(lax.all_to_all(outgoing[0], 'outer', split_axis=0, concat_...  42.1 us
    all_to_all x1, blocking collectives, shards(): lax.all_to_all(outgoing[2], 'outer', split_axis=0, concat_axis=3, tiled=T...  30.9 us
  transfers between devices with their start and end apart: 11, of which 9 were waited for; matrix products, arithmetic and copies ran while one was open for 15% of the time, Pallas kernels for 0%

commit v1 on v0

--- a/solution.py
+++ b/solution.py
@@ -1,6 +1,8 @@
 import jax
 import jax.numpy as jnp
 from jax import lax
+from jax.experimental import pallas as pl
+from jax.experimental.pallas import tpu as pltpu
 from jax.sharding import PartitionSpec as P
 
 COARSE = 16
@@ -142,6 +144,264 @@
     rows_back = returned.reshape(total, width)
     return rows_back[flat].reshape(tok_rows, heads, width)
 
+AUX = 16
+
+
+def exchange_kernel(
+    chips, half, tok, slots, x_ref, o_ref, recv, ans, kp, vp, xp, qp, op, vis_ref,
+    send_sem, recv_sem, fsend, frecv, bsend, brecv,
+):
+    f32, bf16 = jnp.float32, jnp.bfloat16
+    width = x_ref.shape[2]
+    inner = lax.axis_index("inner")
+    chip = lax.axis_index("outer") * half + inner // 2
+    core = inner % 2
+    partner = {"outer": lax.axis_index("outer"), "inner": inner + 1 - 2 * core}
+    head_rows = pl.ds(tok, x_ref.shape[1] - tok)
+
+    def at(other):
+        return {"outer": other // half, "inner": (other % half) * 2 + core}
+
+    def copy(src, dst, s1, s2, where):
+        return pltpu.make_async_remote_copy(
+            src_ref=src, dst_ref=dst, send_sem=s1, recv_sem=s2,
+            device_id=where, device_id_type=pl.DeviceIdType.MESH,
+        )
+
+    barrier = pltpu.get_barrier_semaphore()
+
+    @pl.loop(1, chips)
+    def _(d):
+        pl.semaphore_signal(
+            barrier, inc=1, device_id=at((chip + d) % chips),
+            device_id_type=pl.DeviceIdType.MESH,
+        )
+
+    pl.semaphore_signal(
+        barrier, inc=1, device_id=partner, device_id_type=pl.DeviceIdType.MESH
+    )
+    pl.semaphore_wait(barrier, chips)
+
+    def outgoing(d):
+        other = (chip + d) % chips
+        return copy(
+            x_ref.at[other], recv.at[2 * chip + core], send_sem.at[d], recv_sem.at[d], at(other)
+        )
+
+    @pl.loop(1, chips)
+    def _(d):
+        outgoing(d).start()
+
+    def source(d):
+        return (chip + chips - d) % chips
+
+    def own_forward():
+        return copy(
+            x_ref.at[chip, head_rows], recv.at[2 * chip + core, head_rows],
+            fsend.at[0], frecv.at[0], partner,
+        )
+
+    def forward(d):
+        row = 2 * source(d) + core
+        return copy(
+            recv.at[row, head_rows], recv.at[row, head_rows], fsend.at[d], frecv.at[d], partner
+        )
+
+    own_forward().start()
+    recv[2 * chip + core] = x_ref[chip]
+
+    lane = lax.broadcasted_iota(jnp.int32, (tok, width), 1)
+    low = (lane < width // 2).astype(f32).astype(bf16)
+    high = (lane >= width // 2).astype(f32).astype(bf16)
+    key_at = lax.broadcasted_iota(jnp.int32, vis_ref.shape, 1)
+    query_at = lax.broadcasted_iota(jnp.int32, vis_ref.shape, 0)
+    key_order = (key_at // 8) * 4 + key_at % 4
+    query_order = (2 * (query_at // 8) + core) * 4 + query_at % 4
+    same = (key_at // 4) % 2 == (query_at // 4) % 2
+    vis_ref[...] = jnp.where(same & (key_order <= query_order), f32(1.0), f32(0.0))
+    halves = tok // width
+
+    def aux_of(row):
+        return jnp.concatenate(
+            [recv[row, pl.ds(3 * tok + AUX * i, AUX)] for i in range(halves)], axis=1
+        )
+
+    def place(row, with_query):
+        aux = aux_of(row).astype(f32)
+        slot = (aux[2:3] + aux[3:4]).astype(jnp.int32)
+        hit = lax.broadcasted_iota(jnp.int32, (slots, tok), 0) == slot
+        one = jnp.where(hit, f32(1.0), f32(0.0)).astype(bf16)
+        by_key = jnp.where(hit, aux[0:1], f32(0.0)).astype(bf16)
+        by_value = jnp.where(hit, aux[1:2], f32(0.0)).astype(bf16)
+        kp[row] = jnp.dot(one, recv[row, pl.ds(tok, tok)], preferred_element_type=f32)
+        vp[row] = jnp.dot(one, recv[row, pl.ds(2 * tok, tok)], preferred_element_type=f32)
+        xp[row] = jnp.dot(by_key, low, preferred_element_type=f32) + jnp.dot(
+            by_value, high, preferred_element_type=f32
+        )
+        if with_query:
+            qp[row // 2] = jnp.dot(one, recv[row, pl.ds(0, tok)], preferred_element_type=f32)
+
+    place(2 * chip + core, True)
+
+    @pl.loop(1, chips)
+    def _(d):
+        outgoing(d).wait_recv()
+        forward(d).start()
+        place(2 * source(d) + core, True)
+
+        @pl.when(d == 1)
+        def _():
+            own_forward().wait_recv()
+
+        @pl.when(d > 1)
+        def _():
+            forward(d - 1).wait_recv()
+
+        place(2 * source(d - 1) + 1 - core, False)
+
+    forward(chips - 1).wait_recv()
+    place(2 * source(chips - 1) + 1 - core, False)
+
+    sel_lane = lax.broadcasted_iota(jnp.int32, (16, width), 1)
+    sel_row = lax.broadcasted_iota(jnp.int32, (16, width), 0)
+    select = (sel_lane == jnp.where(sel_row < 8, 0, width // 2)).astype(f32).astype(bf16)
+    factor = width ** (-0.5)
+    queries_here, keys_here = vis_ref.shape
+
+    def group(t):
+        rows = pl.ds(pl.multiple_of(t * 8, 8), 8)
+        key = kp[:, rows, :].reshape(keys_here, width).astype(bf16)
+        value = vp[:, rows, :].reshape(keys_here, width).astype(bf16)
+        extra = xp[:, rows, :].reshape(keys_here, width).astype(bf16)
+        query = qp[:, rows, :].reshape(queries_here, width).astype(bf16)
+        nt = (((1,), (1,)), ((), ()))
+        scale = lax.dot_general(select, extra, nt, preferred_element_type=f32)
+        scores = lax.dot_general(query, key, nt, preferred_element_type=f32)
+        scores = scores * (scale[0:1] * factor)
+        visible = vis_ref[...] * scale[0:1] > 0
+        scores = jnp.where(visible, scores, f32(-1e30))
+        highest = jnp.max(scores, axis=1, keepdims=True)
+        unnormed = jnp.where(visible, jnp.exp(scores - highest), f32(0.0))
+        denominator = jnp.sum(unnormed, axis=1, keepdims=True)
+        weights = (unnormed * scale[8:9]).astype(bf16)
+        numerator = jnp.dot(weights, value, preferred_element_type=f32)
+        safe = jnp.where(denominator > 0, denominator, f32(1.0))
+        result = (numerator / safe).astype(bf16).astype(f32)
+        op[:, rows, :] = result.reshape(queries_here // 8, 8, width)
+
+    @pl.loop(0, slots // 8 // UNROLL)
+    def _(t):
+        for u in range(UNROLL):
+            group(t * UNROLL + u)
+
+    eye = (
+        lax.broadcasted_iota(jnp.int32, (tok, tok), 0)
+        == lax.broadcasted_iota(jnp.int32, (tok, tok), 1)
+    ).astype(f32).astype(bf16)
+
+    def answer(other):
+        columns = lax.dot_general(
+            eye, aux_of(2 * other + core), (((1,), (1,)), ((), ())), preferred_element_type=f32
+        )
+        slot = (columns[:, 2:3] + columns[:, 3:4]).astype(jnp.int32)
+        hit = lax.broadcasted_iota(jnp.int32, (tok, slots), 1) == slot
+        one = jnp.where(hit, f32(1.0), f32(0.0)).astype(bf16)
+        return jnp.dot(one, op[other].astype(bf16), preferred_element_type=f32).astype(bf16)
+
+    def reply(d):
+        other = (chip + d) % chips
+        return copy(ans.at[other], o_ref.at[chip], bsend.at[d], brecv.at[d], at(other))
+
+    @pl.loop(1, chips)
+    def _(d):
+        other = (chip + d) % chips
+        ans[other] = answer(other)
+
+        @pl.when(d > 1)
+        def _():
+            reply(d - 1).start()
+
+    o_ref[chip] = answer(chip)
+    reply(chips - 1).start()
+    own_forward().wait_send()
+
+    @pl.loop(1, chips)
+    def _(d):
+        outgoing(d).wait_send()
+        forward(d).wait_send()
+        reply(d).wait()
+
+
+def by_head(queries, key_rows, value_rows, key_scale, value_scale, cluster_label):
+    tok, heads, width = queries.shape
+    half = lax.axis_size("inner") // 2
+    chips = lax.axis_size("outer") * half
+    clusters = COARSE * FINE
+    capacity = max(2, 2 * tok // clusters)
+    slots = clusters * capacity
+    labels = cluster_label[:, :, 0]
+    earlier = jnp.arange(tok)[None, :] < jnp.arange(tok)[:, None]
+    rank = jnp.sum(
+        ((labels[:, :, None] == labels[:, None, :]) & earlier[None]).astype(jnp.int32), axis=2
+    )
+    aux = jnp.stack(
+        [
+            key_scale.T,
+            value_scale.T,
+            (labels * capacity).astype(jnp.bfloat16),
+            rank.astype(jnp.bfloat16),
+        ],
+        axis=1,
+    )
+    aux = jnp.pad(aux, ((0, 0), (0, AUX - 4), (0, 0)))
+    aux = aux.reshape(heads, AUX, tok // width, width).swapaxes(1, 2).reshape(heads, -1, width)
+    packed = jnp.concatenate(
+        [
+            queries.swapaxes(0, 1),
+            key_rows.swapaxes(0, 1),
+            value_rows.swapaxes(0, 1),
+            aux,
+        ],
+        axis=1,
+    )
+    vm = pl.BlockSpec(memory_space=pltpu.VMEM)
+    dma = pltpu.SemaphoreType.DMA
+    f32 = jnp.float32
+    returned = pl.pallas_call(
+        lambda *refs: exchange_kernel(chips, half, tok, slots, *refs),
+        out_shape=jax.ShapeDtypeStruct((heads, tok, width), jnp.bfloat16),
+        in_specs=[vm],
+        out_specs=vm,
+        scratch_shapes=[
+            pltpu.VMEM((2 * chips,) + packed.shape[1:], jnp.bfloat16),
+            pltpu.VMEM((chips, tok, width), jnp.bfloat16),
+            pltpu.VMEM((2 * chips, slots, width), f32),
+            pltpu.VMEM((2 * chips, slots, width), f32),
+            pltpu.VMEM((2 * chips, slots, width), f32),
+            pltpu.VMEM((chips, slots, width), f32),
+            pltpu.VMEM((chips, slots, width), f32),
+            pltpu.VMEM((8 * chips, 16 * chips), f32),
+        ]
+        + [dma((chips,))] * 6,
+        compiler_params=pltpu.CompilerParams(
+            collective_id=0, has_side_effects=True, vmem_limit_bytes=62 * 1024 * 1024
+        ),
+        name="clustered",
+    )(packed)
+    return returned.swapaxes(0, 1)
+
+
+UNROLL = 2
+
+
+def route(queries, key_rows, value_rows, key_scale, value_scale, cluster_label):
+    tok, heads, width = queries.shape
+    devices = lax.axis_size("outer") * lax.axis_size("inner")
+    even = lax.axis_size("inner") % 2 == 0 and tok % width == 0
+    if devices == 2 * heads and even and 2 * tok == 4 * COARSE * FINE:
+        return by_head(queries, key_rows, value_rows, key_scale, value_scale, cluster_label)
+    return shards(queries, key_rows, value_rows, key_scale, value_scale, cluster_label)
+
 
 def solution(mesh):
     placed = (
@@ -153,7 +413,7 @@
         P(None, ("outer", "inner"), None),
     )
     return jax.shard_map(
-        shards,
+        route,
         mesh=mesh,
         in_specs=placed,
         out_specs=P(("outer", "inner"), None, None),

time: 810 us -> 140 us (0.17); the launches traced: 800 us -> 140 us
  local copies, waits for them, and re-layouts: 264 us -> 5.01 us
  waiting for transfers between devices: 192 us -> 0 us
  matrix products: 166 us -> 0 us
  Pallas kernels: 0 us -> 130 us
  blocking collectives: 111 us -> 0 us
  starting transfers between devices: 45.5 us -> 0 us
  other arithmetic: 20.4 us -> 4.74 us
    gather x6 -> x0, local copies, waits for them, and re-layouts: 204 us -> none  [the longest x5 189 us: place(): picked = rows[source_row]]
    all_to_all x11 -> x0, waiting for transfers between devices: 192 us -> none  [the longest x1 45.8 us: shards(): lax.all_to_all(lax.all_to_all(outgoing[2], 'outer', split_axis=0, concat_...]
    dot_general x128 -> x0, matrix products: 166 us -> none  [the longest x64 106 us: attend(): jnp.dot(weights, value_block, preferred_element_type=jnp.float32)]
    pallas_call x0 -> x1, Pallas kernels: none -> 130 us  [by_head(): pl.pallas_call(lambda *refs: exchange_kernel(chips, half, tok, slots, *re...]
    all_to_all x3 -> x0, blocking collectives: 111 us -> none  [the longest x1 51.5 us: shards(): lax.all_to_all(answered, 'inner', split_axis=3, concat_axis=1, tiled=True)]
    all_to_all x11 -> x0, starting transfers between devices: 45.5 us -> none  [the longest x1 5.19 us: shards(): lax.all_to_all(outgoing[3], 'outer', split_axis=0, concat_axis=3, tiled=T...]
    scatter x1 -> x0, local copies, waits for them, and re-layouts: 15.5 us -> none  [shards(): source = jnp.full((total,), -1, jnp.int32).at[flat].set(jnp.arange(tok_ro...]
    all_to_all x10 -> x0, local copies, waits for them, and re-layouts: 13.9 us -> none  [the longest x1 3.21 us: shards(): lax.all_to_all(outgoing[2], 'outer', split_axis=0, concat_axis=3, tiled=T...]
  transfers between devices with their start and end apart: 11 -> 0, of which waited for: 9 -> 0; matrix products, arithmetic and copies ran while one was open for 15% -> 0% of each run, Pallas kernels for 0% -> 0%
where the time goes in v1:
time: 140 us
  Pallas kernels  130 us (93%)
  local copies, waits for them, and re-layouts  5.01 us (4%)
  other arithmetic  4.74 us (3%)
    pallas_call x1, Pallas kernels, by_head(): pl.pallas_call(lambda *refs: exchange_kernel(chips, half, tok, slots, *re...  130 us
    transpose x1, local copies, waits for them, and re-layouts, by_head(): return returned.swapaxes(0, 1)  2.87 us

profile of v1, /device:TPU:0, one launch (start us, length us, event | category | flops | bytes accessed | tf_op | source)
XLA Modules:
  0.0 139.9 jit_solution(11751855865782983377)
XLA Ops:
  0.0 0.0 copy-start
  0.0 0.0 copy-start.1
  0.0 0.9 fusion.7
  0.9 1.3 convert_reduce_fusion
  2.2 0.7 fusion.6
  3.0 0.1 copy.16
  3.1 1.5 %copy.26 = bf16[256,16,128]{2,0,1:T(8,128)(2,1)S(1)} copy(bf16[256,16,128]{2,1,0:T(8,128)(2,1)} %param.6) | data formatting | bytes 2097152 | tf_op args[0]
  4.6 0.0 copy-done
  4.6 0.0 copy-done.1
  4.6 0.5 copy_bitcast_fusion
  5.1 1.8 %pad_maximum_fusion.refs_0_ = bf16[16,800,128]{2,1,0:T(8,128)(2,1)} fusion(bf16[16,32,128]{2,1,0:T(8,128)(2,1)S(1)} %bitcast.27, bf16[16,256,128]{2,1,0:T(8,128)(2,1)S(1)} %get-tuple-element.7, bf16[16,256,128]{2,1,0:T(8,128)(2,1)S(1)} %get-tuple-element.8, bf16[16,256,128]{2,1,0:T(8,128)(2,1)S(1)} %bitcast.25), kind=kLoop, calls=%fused_computation.1 | loop fusion | flops 13107200 | bytes 6553600 | tf_op jit(solution)/shard_map/concatenate | solution.py:358
  6.9 130.1 %clustered.1 = bf16[16,256,128]{2,1,0:T(8,128)(2,1)} custom-call(bf16[16,800,128]{2,1,0:T(8,128)(2,1)} %pad_maximum_fusion.refs_0_), custom_call_target="tpu_custom_call" | custom-call | tf_op jit(solution)/shard_map/clustered/pallas_call | solution.py:370
  137.0 2.9 %copy.17 = bf16[256,16,128]{2,1,0:T(8,128)(2,1)} copy(bf16[256,16,128]{2,0,1:T(8,128)(2,1)} %bitcast.26) | data formatting | bytes 2097152 | tf_op jit(solution)/shard_map/transpose | solution.py:391
  (3 shorter events, 0.1 us)
Async XLA Ops:
  0.0 4.6 %copy-start = (bf16[256,16,128]{2,1,0:T(8,128)(2,1)S(1)}, bf16[256,16,128]{2,1,0:T(8,128)(2,1)}, u32[]{:S(2)}) copy-start(bf16[256,16,128]{2,1,0:T(8,128)(2,1)} %param.8) | copy-start | bytes 3145732
  0.0 4.6 %copy-start.1 = (bf16[256,16,128]{2,1,0:T(8,128)(2,1)S(1)}, bf16[256,16,128]{2,1,0:T(8,128)(2,1)}, u32[]{:S(2)}) copy-start(bf16[256,16,128]{2,1,0:T(8,128)(2,1)} %param.7) | copy-start | bytes 3145732

commit v2 on v1

--- a/solution.py
+++ b/solution.py
@@ -144,12 +144,12 @@
     rows_back = returned.reshape(total, width)
     return rows_back[flat].reshape(tok_rows, heads, width)
 
-AUX = 16
+AUX = 8
 
 
 def exchange_kernel(
-    chips, half, tok, slots, x_ref, o_ref, recv, ans, kp, vp, xp, qp, op, vis_ref,
-    send_sem, recv_sem, fsend, frecv, bsend, brecv,
+    chips, half, tok, slots, x_ref, o_ref, recv, ans, kp, vp, xp, qp, op, held, vis_ref,
+    send_sem, recv_sem, fsend, frecv, vsend, vrecv, vfsend, vfrecv, bsend, brecv,
 ):
     f32, bf16 = jnp.float32, jnp.bfloat16
     width = x_ref.shape[2]
@@ -157,7 +157,8 @@
     chip = lax.axis_index("outer") * half + inner // 2
     core = inner % 2
     partner = {"outer": lax.axis_index("outer"), "inner": inner + 1 - 2 * core}
-    head_rows = pl.ds(tok, x_ref.shape[1] - tok)
+    first = x_ref.shape[1] - tok
+    first_rows, key_rows, value_rows = pl.ds(0, first), pl.ds(tok, first - tok), pl.ds(first, tok)
 
     def at(other):
         return {"outer": other // half, "inner": (other % half) * 2 + core}
@@ -185,29 +186,40 @@
     def outgoing(d):
         other = (chip + d) % chips
         return copy(
-            x_ref.at[other], recv.at[2 * chip + core], send_sem.at[d], recv_sem.at[d], at(other)
+            x_ref.at[other, first_rows], recv.at[2 * chip + core, first_rows],
+            send_sem.at[d], recv_sem.at[d], at(other),
+        )
+
+    def outgoing_value(d):
+        other = (chip + d) % chips
+        return copy(
+            x_ref.at[other, value_rows], recv.at[2 * chip + core, value_rows],
+            vsend.at[d], vrecv.at[d], at(other),
         )
 
     @pl.loop(1, chips)
     def _(d):
         outgoing(d).start()
+
+    @pl.loop(1, chips)
+    def _(d):
+        outgoing_value(d).start()
 
     def source(d):
         return (chip + chips - d) % chips
 
-    def own_forward():
+    def own_forward(rows, s1, s2):
         return copy(
-            x_ref.at[chip, head_rows], recv.at[2 * chip + core, head_rows],
-            fsend.at[0], frecv.at[0], partner,
-        )
-
-    def forward(d):
+            x_ref.at[chip, rows], recv.at[2 * chip + core, rows], s1.at[0], s2.at[0], partner
+        )
+
+    def forward(d, rows, s1, s2):
         row = 2 * source(d) + core
-        return copy(
-            recv.at[row, head_rows], recv.at[row, head_rows], fsend.at[d], frecv.at[d], partner
-        )
-
-    own_forward().start()
+        return copy(recv.at[row, rows], recv.at[row, rows], s1.at[d], s2.at[d], partner)
+
+    by_keys, by_values = (key_rows, fsend, frecv), (value_rows, vfsend, vfrecv)
+    own_forward(*by_keys).start()
+    own_forward(*by_values).start()
     recv[2 * chip + core] = x_ref[chip]
 
     lane = lax.broadcasted_iota(jnp.int32, (tok, width), 1)
@@ -222,44 +234,51 @@
     halves = tok // width
 
     def aux_of(row):
+        block = recv[row, pl.ds(2 * tok, AUX * halves)].astype(f32)
         return jnp.concatenate(
-            [recv[row, pl.ds(3 * tok + AUX * i, AUX)] for i in range(halves)], axis=1
-        )
+            [block[AUX * i : AUX * (i + 1)] for i in range(halves)], axis=1
+        )
+
+    def hits(aux):
+        slot = (aux[2:3] + aux[3:4]).astype(jnp.int32)
+        return lax.broadcasted_iota(jnp.int32, (slots, tok), 0) == slot
 
     def place(row, with_query):
-        aux = aux_of(row).astype(f32)
-        slot = (aux[2:3] + aux[3:4]).astype(jnp.int32)
-        hit = lax.broadcasted_iota(jnp.int32, (slots, tok), 0) == slot
+        aux = aux_of(row)
+        hit = hits(aux)
         one = jnp.where(hit, f32(1.0), f32(0.0)).astype(bf16)
         by_key = jnp.where(hit, aux[0:1], f32(0.0)).astype(bf16)
         by_value = jnp.where(hit, aux[1:2], f32(0.0)).astype(bf16)
         kp[row] = jnp.dot(one, recv[row, pl.ds(tok, tok)], preferred_element_type=f32)
-        vp[row] = jnp.dot(one, recv[row, pl.ds(2 * tok, tok)], preferred_element_type=f32)
         xp[row] = jnp.dot(by_key, low, preferred_element_type=f32) + jnp.dot(
             by_value, high, preferred_element_type=f32
         )
         if with_query:
             qp[row // 2] = jnp.dot(one, recv[row, pl.ds(0, tok)], preferred_element_type=f32)
 
+    def place_value(row):
+        one = jnp.where(hits(aux_of(row)), f32(1.0), f32(0.0)).astype(bf16)
+        vp[row] = jnp.dot(one, recv[row, value_rows], preferred_element_type=f32)
+
     place(2 * chip + core, True)
 
     @pl.loop(1, chips)
     def _(d):
         outgoing(d).wait_recv()
-        forward(d).start()
+        forward(d, *by_keys).start()
         place(2 * source(d) + core, True)
 
         @pl.when(d == 1)
         def _():
-            own_forward().wait_recv()
+            own_forward(*by_keys).wait_recv()
 
         @pl.when(d > 1)
         def _():
-            forward(d - 1).wait_recv()
+            forward(d - 1, *by_keys).wait_recv()
 
         place(2 * source(d - 1) + 1 - core, False)
 
-    forward(chips - 1).wait_recv()
+    forward(chips - 1, *by_keys).wait_recv()
     place(2 * source(chips - 1) + 1 - core, False)
 
     sel_lane = lax.broadcasted_iota(jnp.int32, (16, width), 1)
@@ -268,10 +287,12 @@
     factor = width ** (-0.5)
     queries_here, keys_here = vis_ref.shape
 
-    def group(t):
-        rows = pl.ds(pl.multiple_of(t * 8, 8), 8)
+    def rows_of(t):
+        return pl.ds(pl.multiple_of(t * 8, 8), 8)
+
+    def score(t):
+        rows = rows_of(t)
         key = kp[:, rows, :].reshape(keys_here, width).astype(bf16)
-        value = vp[:, rows, :].reshape(keys_here, width).astype(bf16)
         extra = xp[:, rows, :].reshape(keys_here, width).astype(bf16)
         query = qp[:, rows, :].reshape(queries_here, width).astype(bf16)
         nt = (((1,), (1,)), ((), ()))
@@ -283,16 +304,53 @@
         highest = jnp.max(scores, axis=1, keepdims=True)
         unnormed = jnp.where(visible, jnp.exp(scores - highest), f32(0.0))
         denominator = jnp.sum(unnormed, axis=1, keepdims=True)
-        weights = (unnormed * scale[8:9]).astype(bf16)
-        numerator = jnp.dot(weights, value, preferred_element_type=f32)
+        held[t] = (unnormed * scale[8:9]).astype(bf16)
         safe = jnp.where(denominator > 0, denominator, f32(1.0))
-        result = (numerator / safe).astype(bf16).astype(f32)
-        op[:, rows, :] = result.reshape(queries_here // 8, 8, width)
-
-    @pl.loop(0, slots // 8 // UNROLL)
+        op[:, rows, :] = jnp.broadcast_to(safe, (queries_here, width)).reshape(
+            queries_here // 8, 8, width
+        )
+
+    def weigh(t):
+        rows = rows_of(t)
+        value = vp[:, rows, :].reshape(keys_here, width).astype(bf16)
+        numerator = jnp.dot(held[t], value, preferred_element_type=f32)
+        result = numerator / op[:, rows, :].reshape(queries_here, width)
+        op[:, rows, :] = result.astype(bf16).astype(f32).reshape(queries_here // 8, 8, width)
+
+    groups = slots // 8
+    step = groups // chips
+
+    def score_some(d):
+        for u in range(step):
+            score(d * step + u)
+
+    score_some(0)
+    place_value(2 * chip + core)
+
+    @pl.loop(1, chips)
+    def _(d):
+        score_some(d)
+        outgoing_value(d).wait_recv()
+        forward(d, *by_values).start()
+        place_value(2 * source(d) + core)
+
+        @pl.when(d == 1)
+        def _():
+            own_forward(*by_values).wait_recv()
+
+        @pl.when(d > 1)
+        def _():
+            forward(d - 1, *by_values).wait_recv()
+
+        place_value(2 * source(d - 1) + 1 - core)
+
+    forward(chips - 1, *by_values).wait_recv()
+    place_value(2 * source(chips - 1) + 1 - core)
+
+    @pl.loop(0, groups // UNROLL)
     def _(t):
         for u in range(UNROLL):
-            group(t * UNROLL + u)
+            weigh(t * UNROLL + u)
 
     eye = (
         lax.broadcasted_iota(jnp.int32, (tok, tok), 0)
@@ -301,7 +359,10 @@
 
     def answer(other):
         columns = lax.dot_general(
-            eye, aux_of(2 * other + core), (((1,), (1,)), ((), ())), preferred_element_type=f32
+            eye,
+            aux_of(2 * other + core).astype(bf16),
+            (((1,), (1,)), ((), ())),
+            preferred_element_type=f32,
         )
         slot = (columns[:, 2:3] + columns[:, 3:4]).astype(jnp.int32)
         hit = lax.broadcasted_iota(jnp.int32, (tok, slots), 1) == slot
@@ -323,12 +384,15 @@
 
     o_ref[chip] = answer(chip)
     reply(chips - 1).start()
-    own_forward().wait_send()
+    own_forward(*by_keys).wait_send()
+    own_forward(*by_values).wait_send()
 
     @pl.loop(1, chips)
     def _(d):
         outgoing(d).wait_send()
-        forward(d).wait_send()
+        outgoing_value(d).wait_send()
+        forward(d, *by_keys).wait_send()
+        forward(d, *by_values).wait_send()
         reply(d).wait()
 
 
@@ -359,8 +423,8 @@
         [
             queries.swapaxes(0, 1),
             key_rows.swapaxes(0, 1),
+            aux,
             value_rows.swapaxes(0, 1),
-            aux,
         ],
         axis=1,
     )
@@ -380,9 +444,10 @@
             pltpu.VMEM((2 * chips, slots, width), f32),
             pltpu.VMEM((chips, slots, width), f32),
             pltpu.VMEM((chips, slots, width), f32),
+            pltpu.VMEM((slots // 8, 8 * chips, 16 * chips), jnp.bfloat16),
             pltpu.VMEM((8 * chips, 16 * chips), f32),
         ]
-        + [dma((chips,))] * 6,
+        + [dma((chips,))] * 10,
         compiler_params=pltpu.CompilerParams(
             collective_id=0, has_side_effects=True, vmem_limit_bytes=62 * 1024 * 1024
         ),
@@ -391,13 +456,13 @@
     return returned.swapaxes(0, 1)
 
 
-UNROLL = 2
+UNROLL = 4
 
 
 def route(queries, key_rows, value_rows, key_scale, value_scale, cluster_label):
     tok, heads, width = queries.shape
     devices = lax.axis_size("outer") * lax.axis_size("inner")
-    even = lax.axis_size("inner") % 2 == 0 and tok % width == 0
+    even = lax.axis_size("inner") % 2 == 0 and tok == 2 * width
     if devices == 2 * heads and even and 2 * tok == 4 * COARSE * FINE:
         return by_head(queries, key_rows, value_rows, key_scale, value_scale, cluster_label)
     return shards(queries, key_rows, value_rows, key_scale, value_scale, cluster_label)

time: 140 us -> 128 us (0.914)
  Pallas kernels: 130 us -> 118 us
    pallas_call x1, Pallas kernels: 130 us -> 118 us  [by_head(): pl.pallas_call(lambda *refs: exchange_kernel(chips, half, tok, slots, *re...]
where the time goes in v2:
time: 128 us
  Pallas kernels  118 us (92%)
  local copies, waits for them, and re-layouts  4.97 us (4%)
  other arithmetic  4.73 us (4%)
    pallas_call x1, Pallas kernels, by_head(): pl.pallas_call(lambda *refs: exchange_kernel(chips, half, tok, slots, *re...  118 us
    transpose x1, local copies, waits for them, and re-layouts, by_head(): return returned.swapaxes(0, 1)  2.87 us

profile of v2, /device:TPU:0, one launch (start us, length us, event | category | flops | bytes accessed | tf_op | source)
XLA Modules:
  0.0 127.6 jit_solution(10596785377011488779)
XLA Ops:
  0.0 0.0 copy-start
  0.0 0.0 copy-start.1
  0.0 0.9 fusion.7
  0.9 1.3 %convert_reduce_fusion = s32[16,256]{1,0:T(8,128)S(1)} fusion(s32[16,256]{1,0:T(8,128)S(1)} %get-tuple-element.6, pred[256,256]{1,0:T(8,128)(4,1)S(1)} %iota_compare_fusion), kind=kLoop, calls=%fused_computation | loop fusion | flops 4190208 | bytes 98304 | tf_op jit(solution)/shard_map/reduce_sum | solution.py:408
  2.2 0.7 fusion.6
  3.0 1.5 %copy.27 = bf16[256,16,128]{2,0,1:T(8,128)(2,1)S(1)} copy(bf16[256,16,128]{2,1,0:T(8,128)(2,1)} %param.6) | data formatting | bytes 2097152 | tf_op args[0]
  4.5 0.0 copy-done
  4.5 0.0 copy-done.1
  4.5 0.5 copy_bitcast_fusion
  5.1 1.8 %pad_maximum_fusion.refs_0_ = bf16[16,784,128]{2,1,0:T(8,128)(2,1)} fusion(bf16[16,256,128]{2,1,0:T(8,128)(2,1)S(1)} %get-tuple-element.7, bf16[16,16,128]{2,1,0:T(8,128)(2,1)S(1)} %bitcast.29, bf16[16,256,128]{2,1,0:T(8,128)(2,1)S(1)} %get-tuple-element.8, bf16[16,256,128]{2,1,0:T(8,128)(2,1)S(1)} %bitcast.27), kind=kLoop, calls=%fused_computation.1 | loop fusion | flops 12845056 | bytes 6422528 | tf_op jit(solution)/shard_map/concatenate | solution.py:422
  6.9 117.8 %clustered.1 = bf16[16,256,128]{2,1,0:T(8,128)(2,1)} custom-call(bf16[16,784,128]{2,1,0:T(8,128)(2,1)} %pad_maximum_fusion.refs_0_), custom_call_target="tpu_custom_call" | custom-call | tf_op jit(solution)/shard_map/clustered/pallas_call | solution.py:434
  124.7 2.9 %copy.17 = bf16[256,16,128]{2,1,0:T(8,128)(2,1)} copy(bf16[256,16,128]{2,0,1:T(8,128)(2,1)} %bitcast.28) | data formatting | bytes 2097152 | tf_op jit(solution)/shard_map/transpose | solution.py:456
  (4 shorter events, 0.1 us)
Async XLA Ops:
  0.0 4.5 %copy-start = (bf16[256,16,128]{2,1,0:T(8,128)(2,1)S(1)}, bf16[256,16,128]{2,1,0:T(8,128)(2,1)}, u32[]{:S(2)}) copy-start(bf16[256,16,128]{2,1,0:T(8,128)(2,1)} %param.8) | copy-start | bytes 3145732
  0.0 4.5 %copy-start.1 = (bf16[256,16,128]{2,1,0:T(8,128)(2,1)S(1)}, bf16[256,16,128]{2,1,0:T(8,128)(2,1)}, u32[]{:S(2)}) copy-start(bf16[256,16,128]{2,1,0:T(8,128)(2,1)} %param.7) | copy-start | bytes 3145732

commit v3 on v1

--- a/solution.py
+++ b/solution.py
@@ -144,12 +144,12 @@
     rows_back = returned.reshape(total, width)
     return rows_back[flat].reshape(tok_rows, heads, width)
 
-AUX = 16
+AUX = 8
 
 
 def exchange_kernel(
-    chips, half, tok, slots, x_ref, o_ref, recv, ans, kp, vp, xp, qp, op, vis_ref,
-    send_sem, recv_sem, fsend, frecv, bsend, brecv,
+    chips, half, tok, slots, x_ref, o_ref, recv, ans, kp, vp, xp, qp, op, kb, vb, scales, vis_ref,
+    send_sem, recv_sem, fsend, frecv, qsend, qrecv, bsend, brecv,
 ):
     f32, bf16 = jnp.float32, jnp.bfloat16
     width = x_ref.shape[2]
@@ -157,7 +157,8 @@
     chip = lax.axis_index("outer") * half + inner // 2
     core = inner % 2
     partner = {"outer": lax.axis_index("outer"), "inner": inner + 1 - 2 * core}
-    head_rows = pl.ds(tok, x_ref.shape[1] - tok)
+    first = x_ref.shape[1] - tok
+    first_rows, query_rows = pl.ds(0, first), pl.ds(first, tok)
 
     def at(other):
         return {"outer": other // half, "inner": (other % half) * 2 + core}
@@ -183,28 +184,37 @@
     pl.semaphore_wait(barrier, chips)
 
     def outgoing(d):
-        other = (chip + d) % chips
+        other = chip ^ d
         return copy(
-            x_ref.at[other], recv.at[2 * chip + core], send_sem.at[d], recv_sem.at[d], at(other)
+            x_ref.at[other, first_rows], recv.at[2 * chip + core, first_rows],
+            send_sem.at[d], recv_sem.at[d], at(other),
+        )
+
+    def outgoing_query(d):
+        other = chip ^ d
+        return copy(
+            x_ref.at[other, query_rows], recv.at[2 * chip + core, query_rows],
+            qsend.at[d], qrecv.at[d], at(other),
         )
 
     @pl.loop(1, chips)
     def _(d):
         outgoing(d).start()
 
-    def source(d):
-        return (chip + chips - d) % chips
+    @pl.loop(1, chips)
+    def _(d):
+        outgoing_query(d).start()
 
     def own_forward():
         return copy(
-            x_ref.at[chip, head_rows], recv.at[2 * chip + core, head_rows],
+            x_ref.at[chip, first_rows], recv.at[2 * chip + core, first_rows],
             fsend.at[0], frecv.at[0], partner,
         )
 
     def forward(d):
-        row = 2 * source(d) + core
+        row = 2 * (chip ^ d) + core
         return copy(
-            recv.at[row, head_rows], recv.at[row, head_rows], fsend.at[d], frecv.at[d], partner
+            recv.at[row, first_rows], recv.at[row, first_rows], fsend.at[d], frecv.at[d], partner
         )
 
     own_forward().start()
@@ -222,32 +232,43 @@
     halves = tok // width
 
     def aux_of(row):
+        block = recv[row, pl.ds(2 * tok, AUX * halves)].astype(f32)
         return jnp.concatenate(
-            [recv[row, pl.ds(3 * tok + AUX * i, AUX)] for i in range(halves)], axis=1
-        )
-
-    def place(row, with_query):
-        aux = aux_of(row).astype(f32)
+            [block[AUX * i : AUX * (i + 1)] for i in range(halves)], axis=1
+        )
+
+    def hits(aux):
         slot = (aux[2:3] + aux[3:4]).astype(jnp.int32)
-        hit = lax.broadcasted_iota(jnp.int32, (slots, tok), 0) == slot
-        one = jnp.where(hit, f32(1.0), f32(0.0)).astype(bf16)
+        return lax.broadcasted_iota(jnp.int32, (slots, tok), 0) == slot
+
+    def one_hot(hit):
+        return jnp.where(hit, f32(1.0), f32(0.0)).astype(bf16)
+
+    def place(row):
+        aux = aux_of(row)
+        hit = hits(aux)
+        one = one_hot(hit)
         by_key = jnp.where(hit, aux[0:1], f32(0.0)).astype(bf16)
         by_value = jnp.where(hit, aux[1:2], f32(0.0)).astype(bf16)
-        kp[row] = jnp.dot(one, recv[row, pl.ds(tok, tok)], preferred_element_type=f32)
-        vp[row] = jnp.dot(one, recv[row, pl.ds(2 * tok, tok)], preferred_element_type=f32)
+        kp[row] = jnp.dot(one, recv[row, pl.ds(0, tok)], preferred_element_type=f32)
+        vp[row] = jnp.dot(one, recv[row, pl.ds(tok, tok)], preferred_element_type=f32)
         xp[row] = jnp.dot(by_key, low, preferred_element_type=f32) + jnp.dot(
             by_value, high, preferred_element_type=f32
         )
-        if with_query:
-            qp[row // 2] = jnp.dot(one, recv[row, pl.ds(0, tok)], preferred_element_type=f32)
-
-    place(2 * chip + core, True)
+
+    def place_query(other):
+        row = 2 * other + core
+        qp[other] = jnp.dot(
+            one_hot(hits(aux_of(row))), recv[row, query_rows], preferred_element_type=f32
+        )
+
+    place(2 * chip + core)
 
     @pl.loop(1, chips)
     def _(d):
         outgoing(d).wait_recv()
         forward(d).start()
-        place(2 * source(d) + core, True)
+        place(2 * (chip ^ d) + core)
 
         @pl.when(d == 1)
         def _():
@@ -257,42 +278,49 @@
         def _():
             forward(d - 1).wait_recv()
 
-        place(2 * source(d - 1) + 1 - core, False)
+        place(2 * (chip ^ (d - 1)) + 1 - core)
 
     forward(chips - 1).wait_recv()
-    place(2 * source(chips - 1) + 1 - core, False)
+    place(2 * (chip ^ (chips - 1)) + 1 - core)
 
     sel_lane = lax.broadcasted_iota(jnp.int32, (16, width), 1)
     sel_row = lax.broadcasted_iota(jnp.int32, (16, width), 0)
     select = (sel_lane == jnp.where(sel_row < 8, 0, width // 2)).astype(f32).astype(bf16)
     factor = width ** (-0.5)
-    queries_here, keys_here = vis_ref.shape
-
-    def group(t):
-        rows = pl.ds(pl.multiple_of(t * 8, 8), 8)
-        key = kp[:, rows, :].reshape(keys_here, width).astype(bf16)
-        value = vp[:, rows, :].reshape(keys_here, width).astype(bf16)
-        extra = xp[:, rows, :].reshape(keys_here, width).astype(bf16)
-        query = qp[:, rows, :].reshape(queries_here, width).astype(bf16)
-        nt = (((1,), (1,)), ((), ()))
-        scale = lax.dot_general(select, extra, nt, preferred_element_type=f32)
-        scores = lax.dot_general(query, key, nt, preferred_element_type=f32)
+    keys_here = vis_ref.shape[1]
+    chunk_rows = CHUNK * 8
+    nt = (((1,), (1,)), ((), ()))
+
+    def rows_of(t):
+        return pl.ds(pl.multiple_of(t * 8, 8), 8)
+
+    @pl.loop(0, slots // 8 // UNROLL)
+    def _(at_group):
+        for u in range(UNROLL):
+            t = at_group * UNROLL + u
+            rows = rows_of(t)
+            kb[t] = kp[:, rows, :].reshape(keys_here, width).astype(bf16)
+            vb[t] = vp[:, rows, :].reshape(keys_here, width).astype(bf16)
+            extra = xp[:, rows, :].reshape(keys_here, width).astype(bf16)
+            scales[t] = lax.dot_general(select, extra, nt, preferred_element_type=f32)
+
+    def group(base, t):
+        here, rows = pl.ds(base, CHUNK), rows_of(t)
+        scale = scales[t]
+        query = qp[here, rows, :].reshape(chunk_rows, width).astype(bf16)
+        scores = lax.dot_general(query, kb[t], nt, preferred_element_type=f32)
         scores = scores * (scale[0:1] * factor)
-        visible = vis_ref[...] * scale[0:1] > 0
+        allowed = vis_ref[pl.ds(pl.multiple_of(base * 8, chunk_rows), chunk_rows), :]
+        visible = allowed * scale[0:1] > 0
         scores = jnp.where(visible, scores, f32(-1e30))
         highest = jnp.max(scores, axis=1, keepdims=True)
         unnormed = jnp.where(visible, jnp.exp(scores - highest), f32(0.0))
         denominator = jnp.sum(unnormed, axis=1, keepdims=True)
         weights = (unnormed * scale[8:9]).astype(bf16)
-        numerator = jnp.dot(weights, value, preferred_element_type=f32)
+        numerator = jnp.dot(weights, vb[t], preferred_element_type=f32)
         safe = jnp.where(denominator > 0, denominator, f32(1.0))
         result = (numerator / safe).astype(bf16).astype(f32)
-        op[:, rows, :] = result.reshape(queries_here // 8, 8, width)
-
-    @pl.loop(0, slots // 8 // UNROLL)
-    def _(t):
-        for u in range(UNROLL):
-            group(t * UNROLL + u)
+        op[here, rows, :] = result.reshape(CHUNK, 8, width)
 
     eye = (
         lax.broadcasted_iota(jnp.int32, (tok, tok), 0)
@@ -301,7 +329,10 @@
 
     def answer(other):
         columns = lax.dot_general(
-            eye, aux_of(2 * other + core), (((1,), (1,)), ((), ())), preferred_element_type=f32
+            eye,
+            aux_of(2 * other + core).astype(bf16),
+            (((1,), (1,)), ((), ())),
+            preferred_element_type=f32,
         )
         slot = (columns[:, 2:3] + columns[:, 3:4]).astype(jnp.int32)
         hit = lax.broadcasted_iota(jnp.int32, (tok, slots), 1) == slot
@@ -309,25 +340,46 @@
         return jnp.dot(one, op[other].astype(bf16), preferred_element_type=f32).astype(bf16)
 
     def reply(d):
-        other = (chip + d) % chips
+        other = chip ^ d
         return copy(ans.at[other], o_ref.at[chip], bsend.at[d], brecv.at[d], at(other))
 
-    @pl.loop(1, chips)
-    def _(d):
-        other = (chip + d) % chips
-        ans[other] = answer(other)
-
-        @pl.when(d > 1)
-        def _():
-            reply(d - 1).start()
+    def finish(first_d, last_d):
+        @pl.loop(first_d, last_d)
+        def _(d):
+            other = chip ^ d
+            ans[other] = answer(other)
+
+            @pl.when(d > first_d)
+            def _():
+                reply(d - 1).start()
+
+        reply(last_d - 1).start()
+
+    place_query(chip)
+    for part in range(chips // CHUNK):
+        first_d = part * CHUNK
+
+        @pl.loop(max(first_d, 1), first_d + CHUNK)
+        def _(d):
+            outgoing_query(d).wait_recv()
+            place_query(chip ^ d)
+
+        base = (chip // CHUNK ^ part) * CHUNK
+
+        @pl.loop(0, slots // 8 // UNROLL)
+        def _(at_group):
+            for u in range(UNROLL):
+                group(base, at_group * UNROLL + u)
+
+        finish(max(first_d, 1), first_d + CHUNK)
 
     o_ref[chip] = answer(chip)
-    reply(chips - 1).start()
     own_forward().wait_send()
 
     @pl.loop(1, chips)
     def _(d):
         outgoing(d).wait_send()
+        outgoing_query(d).wait_send()
         forward(d).wait_send()
         reply(d).wait()
 
@@ -357,10 +409,10 @@
     aux = aux.reshape(heads, AUX, tok // width, width).swapaxes(1, 2).reshape(heads, -1, width)
     packed = jnp.concatenate(
         [
-            queries.swapaxes(0, 1),
             key_rows.swapaxes(0, 1),
             value_rows.swapaxes(0, 1),
             aux,
+            queries.swapaxes(0, 1),
         ],
         axis=1,
     )
@@ -380,9 +432,12 @@
             pltpu.VMEM((2 * chips, slots, width), f32),
             pltpu.VMEM((chips, slots, width), f32),
             pltpu.VMEM((chips, slots, width), f32),
+            pltpu.VMEM((slots // 8, 16 * chips, width), jnp.bfloat16),
+            pltpu.VMEM((slots // 8, 16 * chips, width), jnp.bfloat16),
+            pltpu.VMEM((slots // 8, 16, 16 * chips), f32),
             pltpu.VMEM((8 * chips, 16 * chips), f32),
         ]
-        + [dma((chips,))] * 6,
+        + [dma((chips,))] * 8,
         compiler_params=pltpu.CompilerParams(
             collective_id=0, has_side_effects=True, vmem_limit_bytes=62 * 1024 * 1024
         ),
@@ -391,13 +446,15 @@
     return returned.swapaxes(0, 1)
 
 
-UNROLL = 2
+UNROLL = 4
+CHUNK = 4
 
 
 def route(queries, key_rows, value_rows, key_scale, value_scale, cluster_label):
     tok, heads, width = queries.shape
     devices = lax.axis_size("outer") * lax.axis_size("inner")
-    even = lax.axis_size("inner") % 2 == 0 and tok % width == 0
+    even = lax.axis_size("inner") % 2 == 0 and tok == 2 * width
+    even = even and heads & (heads - 1) == 0 and heads % CHUNK == 0
     if devices == 2 * heads and even and 2 * tok == 4 * COARSE * FINE:
         return by_head(queries, key_rows, value_rows, key_scale, value_scale, cluster_label)
     return shards(queries, key_rows, value_rows, key_scale, value_scale, cluster_label)

time: 140 us -> 175 us (1.25)
  Pallas kernels: 130 us -> 165 us
    pallas_call x1, Pallas kernels: 130 us -> 165 us  [by_head(): pl.pallas_call(lambda *refs: exchange_kernel(chips, half, tok, slots, *re...]
where the time goes in v3:
time: 175 us; the launch traced here: 174 us
  Pallas kernels  165 us (94%)
  local copies, waits for them, and re-layouts  4.97 us (3%)
  other arithmetic  4.73 us (3%)
    pallas_call x1, Pallas kernels, by_head(): pl.pallas_call(lambda *refs: exchange_kernel(chips, half, tok, slots, *re...  165 us

profile of v3, /device:TPU:0, one launch (start us, length us, event | category | flops | bytes accessed | tf_op | source)
XLA Modules:
  0.0 174.3 jit_solution(3783653725148008883)
XLA Ops:
  0.0 0.0 copy-start.1
  0.0 0.0 copy-start
  0.0 0.9 fusion.7
  0.9 1.3 convert_reduce_fusion
  2.2 0.7 fusion.6
  3.0 1.5 copy.27
  4.5 0.0 copy-done.1
  4.5 0.0 copy-done
  4.5 0.5 copy_bitcast_fusion
  5.1 1.8 %pad_maximum_fusion.refs_0_ = bf16[16,784,128]{2,1,0:T(8,128)(2,1)} fusion(bf16[16,256,128]{2,1,0:T(8,128)(2,1)S(1)} %get-tuple-element.7, bf16[16,16,128]{2,1,0:T(8,128)(2,1)S(1)} %bitcast.29, bf16[16,256,128]{2,1,0:T(8,128)(2,1)S(1)} %get-tuple-element.8, bf16[16,256,128]{2,1,0:T(8,128)(2,1)S(1)} %bitcast.27), kind=kLoop, calls=%fused_computation.1 | loop fusion | flops 12845056 | bytes 6422528 | tf_op jit(solution)/shard_map/concatenate | solution.py:410
  6.9 164.6 %clustered.1 = bf16[16,256,128]{2,1,0:T(8,128)(2,1)} custom-call(bf16[16,784,128]{2,1,0:T(8,128)(2,1)} %pad_maximum_fusion.refs_0_), custom_call_target="tpu_custom_call" | custom-call | tf_op jit(solution)/shard_map/clustered/pallas_call | solution.py:422
  171.5 2.9 %copy.17 = bf16[256,16,128]{2,1,0:T(8,128)(2,1)} copy(bf16[256,16,128]{2,0,1:T(8,128)(2,1)} %bitcast.28) | data formatting | bytes 2097152 | tf_op jit(solution)/shard_map/transpose | solution.py:446
  (4 shorter events, 0.1 us)
Async XLA Ops:
  0.0 4.5 %copy-start.1 = (bf16[256,16,128]{2,1,0:T(8,128)(2,1)S(1)}, bf16[256,16,128]{2,1,0:T(8,128)(2,1)}, u32[]{:S(2)}) copy-start(bf16[256,16,128]{2,1,0:T(8,128)(2,1)} %param.8) | copy-start | bytes 3145732
  0.0 4.5 %copy-start = (bf16[256,16,128]{2,1,0:T(8,128)(2,1)S(1)}, bf16[256,16,128]{2,1,0:T(8,128)(2,1)}, u32[]{:S(2)}) copy-start(bf16[256,16,128]{2,1,0:T(8,128)(2,1)} %param.6) | copy-start | bytes 3145732

commit v4 on v3

--- a/solution.py
+++ b/solution.py
@@ -304,23 +304,34 @@
             extra = xp[:, rows, :].reshape(keys_here, width).astype(bf16)
             scales[t] = lax.dot_general(select, extra, nt, preferred_element_type=f32)
 
-    def group(base, t):
-        here, rows = pl.ds(base, CHUNK), rows_of(t)
-        scale = scales[t]
-        query = qp[here, rows, :].reshape(chunk_rows, width).astype(bf16)
-        scores = lax.dot_general(query, kb[t], nt, preferred_element_type=f32)
-        scores = scores * (scale[0:1] * factor)
+    def attend_groups(base, groups):
+        here = pl.ds(base, CHUNK)
         allowed = vis_ref[pl.ds(pl.multiple_of(base * 8, chunk_rows), chunk_rows), :]
-        visible = allowed * scale[0:1] > 0
-        scores = jnp.where(visible, scores, f32(-1e30))
-        highest = jnp.max(scores, axis=1, keepdims=True)
-        unnormed = jnp.where(visible, jnp.exp(scores - highest), f32(0.0))
-        denominator = jnp.sum(unnormed, axis=1, keepdims=True)
-        weights = (unnormed * scale[8:9]).astype(bf16)
-        numerator = jnp.dot(weights, vb[t], preferred_element_type=f32)
-        safe = jnp.where(denominator > 0, denominator, f32(1.0))
-        result = (numerator / safe).astype(bf16).astype(f32)
-        op[here, rows, :] = result.reshape(CHUNK, 8, width)
+        scale = [scales[t] for t in groups]
+        query = [qp[here, rows_of(t), :].reshape(chunk_rows, width).astype(bf16) for t in groups]
+        scores = [
+            lax.dot_general(q, kb[t], nt, preferred_element_type=f32)
+            for q, t in zip(query, groups)
+        ]
+        visible = [allowed * c[0:1] > 0 for c in scale]
+        scores = [
+            jnp.where(ok, s * (c[0:1] * factor), f32(-1e30))
+            for ok, s, c in zip(visible, scores, scale)
+        ]
+        highest = [jnp.max(s, axis=1, keepdims=True) for s in scores]
+        unnormed = [
+            jnp.where(ok, jnp.exp(s - m), f32(0.0))
+            for ok, s, m in zip(visible, scores, highest)
+        ]
+        weights = [(e * c[8:9]).astype(bf16) for e, c in zip(unnormed, scale)]
+        numerator = [
+            jnp.dot(w, vb[t], preferred_element_type=f32) for w, t in zip(weights, groups)
+        ]
+        denominator = [jnp.sum(e, axis=1, keepdims=True) for e in unnormed]
+        safe = [jnp.where(n > 0, n, f32(1.0)) for n in denominator]
+        result = [(n / d).astype(bf16).astype(f32) for n, d in zip(numerator, safe)]
+        for r, t in zip(result, groups):
+            op[here, rows_of(t), :] = r.reshape(CHUNK, 8, width)
 
     eye = (
         lax.broadcasted_iota(jnp.int32, (tok, tok), 0)
@@ -368,8 +379,7 @@
 
         @pl.loop(0, slots // 8 // UNROLL)
         def _(at_group):
-            for u in range(UNROLL):
-                group(base, at_group * UNROLL + u)
+            attend_groups(base, [at_group * UNROLL + u for u in range(UNROLL)])
 
         finish(max(first_d, 1), first_d + CHUNK)
 
@@ -446,8 +456,8 @@
     return returned.swapaxes(0, 1)
 
 
-UNROLL = 4
-CHUNK = 4
+UNROLL = 8
+CHUNK = 8
 
 
 def route(queries, key_rows, value_rows, key_scale, value_scale, cluster_label):

time: 175 us -> 119 us (0.68)
  Pallas kernels: 165 us -> 108 us
    pallas_call x1, Pallas kernels: 165 us -> 108 us  [by_head(): pl.pallas_call(lambda *refs: exchange_kernel(chips, half, tok, slots, *re...]
where the time goes in v4:
time: 119 us; the launch traced here: 118 us
  Pallas kernels  108 us (91%)
  local copies, waits for them, and re-layouts  4.97 us (4%)
  other arithmetic  4.73 us (4%)
    pallas_call x1, Pallas kernels, by_head(): pl.pallas_call(lambda *refs: exchange_kernel(chips, half, tok, slots, *re...  108 us
    transpose x1, local copies, waits for them, and re-layouts, by_head(): return returned.swapaxes(0, 1)  2.87 us

profile of v4, /device:TPU:0, one launch (start us, length us, event | category | flops | bytes accessed | tf_op | source)
XLA Modules:
  0.0 118.2 jit_solution(5692155545850118362)
XLA Ops:
  0.0 0.0 copy-start.1
  0.0 0.0 copy-start
  0.0 0.9 fusion.7
  0.9 1.3 %convert_reduce_fusion = s32[16,256]{1,0:T(8,128)S(1)} fusion(s32[16,256]{1,0:T(8,128)S(1)} %get-tuple-element.6, pred[256,256]{1,0:T(8,128)(4,1)S(1)} %iota_compare_fusion), kind=kLoop, calls=%fused_computation | loop fusion | flops 4190208 | bytes 98304 | tf_op jit(solution)/shard_map/reduce_sum | solution.py:406
  2.2 0.7 fusion.6
  3.0 1.5 %copy.27 = bf16[256,16,128]{2,0,1:T(8,128)(2,1)S(1)} copy(bf16[256,16,128]{2,1,0:T(8,128)(2,1)} %param.7) | data formatting | bytes 2097152 | tf_op args[1]
  4.5 0.0 copy-done.1
  4.5 0.0 copy-done
  4.5 0.5 copy_bitcast_fusion
  5.1 1.8 %pad_maximum_fusion.refs_0_ = bf16[16,784,128]{2,1,0:T(8,128)(2,1)} fusion(bf16[16,256,128]{2,1,0:T(8,128)(2,1)S(1)} %get-tuple-element.7, bf16[16,16,128]{2,1,0:T(8,128)(2,1)S(1)} %bitcast.29, bf16[16,256,128]{2,1,0:T(8,128)(2,1)S(1)} %get-tuple-element.8, bf16[16,256,128]{2,1,0:T(8,128)(2,1)S(1)} %bitcast.27), kind=kLoop, calls=%fused_computation.1 | loop fusion | flops 12845056 | bytes 6422528 | tf_op jit(solution)/shard_map/concatenate | solution.py:420
  6.9 108.4 %clustered.1 = bf16[16,256,128]{2,1,0:T(8,128)(2,1)} custom-call(bf16[16,784,128]{2,1,0:T(8,128)(2,1)} %pad_maximum_fusion.refs_0_), custom_call_target="tpu_custom_call" | custom-call | tf_op jit(solution)/shard_map/clustered/pallas_call | solution.py:432
  115.3 2.9 %copy.17 = bf16[256,16,128]{2,1,0:T(8,128)(2,1)} copy(bf16[256,16,128]{2,0,1:T(8,128)(2,1)} %bitcast.28) | data formatting | bytes 2097152 | tf_op jit(solution)/shard_map/transpose | solution.py:456
  (4 shorter events, 0.1 us)
Async XLA Ops:
  0.0 4.5 %copy-start.1 = (bf16[256,16,128]{2,1,0:T(8,128)(2,1)S(1)}, bf16[256,16,128]{2,1,0:T(8,128)(2,1)}, u32[]{:S(2)}) copy-start(bf16[256,16,128]{2,1,0:T(8,128)(2,1)} %param.8) | copy-start | bytes 3145732
  0.0 4.5 %copy-start = (bf16[256,16,128]{2,1,0:T(8,128)(2,1)S(1)}, bf16[256,16,128]{2,1,0:T(8,128)(2,1)}, u32[]{:S(2)}) copy-start(bf16[256,16,128]{2,1,0:T(8,128)(2,1)} %param.6) | copy-start | bytes 3145732

commit v5 on v4

--- a/solution.py
+++ b/solution.py
@@ -456,8 +456,8 @@
     return returned.swapaxes(0, 1)
 
 
-UNROLL = 8
-CHUNK = 8
+UNROLL = 16
+CHUNK = 4
 
 
 def route(queries, key_rows, value_rows, key_scale, value_scale, cluster_label):

time: 119 us -> 116 us (0.975)
  Pallas kernels: 108 us -> 106 us
    pallas_call x1, Pallas kernels: 108 us -> 106 us  [by_head(): pl.pallas_call(lambda *refs: exchange_kernel(chips, half, tok, slots, *re...]
where the time goes in v5:
time: 116 us
  Pallas kernels  106 us (91%)
  local copies, waits for them, and re-layouts  4.97 us (4%)
  other arithmetic  4.73 us (4%)
    pallas_call x1, Pallas kernels, by_head(): pl.pallas_call(lambda *refs: exchange_kernel(chips, half, tok, slots, *re...  106 us
    transpose x1, local copies, waits for them, and re-layouts, by_head(): return returned.swapaxes(0, 1)  2.87 us

profile of v5, /device:TPU:0, one launch (start us, length us, event | category | flops | bytes accessed | tf_op | source)
XLA Modules:
  0.0 115.6 jit_solution(14027694903336505980)
XLA Ops:
  0.0 0.0 copy-start.1
  0.0 0.0 copy-start
  0.0 0.9 fusion.7
  0.9 1.3 %convert_reduce_fusion = s32[16,256]{1,0:T(8,128)S(1)} fusion(s32[16,256]{1,0:T(8,128)S(1)} %get-tuple-element.6, pred[256,256]{1,0:T(8,128)(4,1)S(1)} %iota_compare_fusion), kind=kLoop, calls=%fused_computation | loop fusion | flops 4190208 | bytes 98304 | tf_op jit(solution)/shard_map/reduce_sum | solution.py:406
  2.2 0.7 fusion.6
  3.0 1.5 %copy.27 = bf16[256,16,128]{2,0,1:T(8,128)(2,1)S(1)} copy(bf16[256,16,128]{2,1,0:T(8,128)(2,1)} %param.7) | data formatting | bytes 2097152 | tf_op args[1]
  4.5 0.0 copy-done.1
  4.5 0.0 copy-done
  4.5 0.5 copy_bitcast_fusion
  5.1 1.8 %pad_maximum_fusion.refs_0_ = bf16[16,784,128]{2,1,0:T(8,128)(2,1)} fusion(bf16[16,256,128]{2,1,0:T(8,128)(2,1)S(1)} %get-tuple-element.7, bf16[16,16,128]{2,1,0:T(8,128)(2,1)S(1)} %bitcast.29, bf16[16,256,128]{2,1,0:T(8,128)(2,1)S(1)} %get-tuple-element.8, bf16[16,256,128]{2,1,0:T(8,128)(2,1)S(1)} %bitcast.27), kind=kLoop, calls=%fused_computation.1 | loop fusion | flops 12845056 | bytes 6422528 | tf_op jit(solution)/shard_map/concatenate | solution.py:420
  6.9 105.8 %clustered.1 = bf16[16,256,128]{2,1,0:T(8,128)(2,1)} custom-call(bf16[16,784,128]{2,1,0:T(8,128)(2,1)} %pad_maximum_fusion.refs_0_), custom_call_target="tpu_custom_call" | custom-call | tf_op jit(solution)/shard_map/clustered/pallas_call | solution.py:432
  112.7 2.9 %copy.17 = bf16[256,16,128]{2,1,0:T(8,128)(2,1)} copy(bf16[256,16,128]{2,0,1:T(8,128)(2,1)} %bitcast.28) | data formatting | bytes 2097152 | tf_op jit(solution)/shard_map/transpose | solution.py:456
  (4 shorter events, 0.1 us)
Async XLA Ops:
  0.0 4.5 %copy-start.1 = (bf16[256,16,128]{2,1,0:T(8,128)(2,1)S(1)}, bf16[256,16,128]{2,1,0:T(8,128)(2,1)}, u32[]{:S(2)}) copy-start(bf16[256,16,128]{2,1,0:T(8,128)(2,1)} %param.8) | copy-start | bytes 3145732
  0.0 4.5 %copy-start = (bf16[256,16,128]{2,1,0:T(8,128)(2,1)S(1)}, bf16[256,16,128]{2,1,0:T(8,128)(2,1)}, u32[]{:S(2)}) copy-start(bf16[256,16,128]{2,1,0:T(8,128)(2,1)} %param.6) | copy-start | bytes 3145732
